TPU v7x, 128 devices: a whole 4x4x4 slice. The times are simulated.
128 devices in a mesh: row: 16 (over z, x), col: 8 (over y, core).
Axes of the slice: x: 4, y: 4, z: 4, core: 2. Of those that a mesh axis runs over, the one named last changes fastest.
Arguments:
- start_block: float32 [8, 131072], P(None, ('row', 'col')), may hold values from -6 to 6
- blocks: bfloat16 [16, 8, 128, 128, 128], P('row', 'col'), as said below
- block_rows: int32 [16, 8, 128], P(None, 'col'), may hold values from 0 to 63, as said below
- block_cols: int32 [16, 8, 128], P(None, 'col'), may hold values from 0 to 127, as said below
- counts: int32 [16, 8], replicated, may hold values from 1 to 128, as said below
Outputs:
- next_block: float32 [8, 131072], P(None, ('row', 'col'))
- tridiagonal: float32 [16, 16], replicated
Inputs may be any that keep to these rules, and one draw needn't show every extreme that they name: `block_rows`: entries of each tile are local block rows below 64; within a tile the used slots name distinct blocks whose global row block is at or after the global column block; slots at or after counts are 0 and not part of H. `block_cols`: local block columns below 128, paired with block_rows; unused slots are 0. `counts`: some tile holds exactly 128 blocks in every draw. Blocks whose global row and column blocks agree are symmetric.
All inputs are finite; a program needn't handle non-finite values.
Results may differ from a plain program's by a relative error of at most 0.0048.
Values may be sent and summed in bfloat16 or wider, within the bound.
A program may use at most 64 MiB of HBM per device.

v0:
```python
import math
import jax
import jax.numpy as jnp
from jax import lax
from jax.sharding import Mesh
from jax.sharding import PartitionSpec as P

ITERS = 2
ROW = ("row_0", "row_1")
COL = ("col_0", "col_1")
ROW_COL = ("row_0", "row_1", "col_0", "col_1")
blocks_per_step = 16


def sent_to_all(value, axis):
    length = lax.axis_size(axis)
    return lax.all_to_all(
        jnp.broadcast_to(value[None], (length, *value.shape)), axis, 0, 0, tiled=True
    )


def joined_along(tiles, dim):
    tiles = jnp.moveaxis(tiles, 0, dim)
    lengths = tiles.shape
    return tiles.reshape(*lengths[:dim], lengths[dim] * lengths[dim + 1], *lengths[dim + 2 :])


def collect(value, axis, dim):
    tiles = sent_to_all(value, axis)
    return joined_along(tiles, dim)


def split_up(value, dim, length):
    lengths = value.shape
    tiles = value.reshape(*lengths[:dim], length, lengths[dim] // length, *lengths[dim + 1 :])
    return jnp.moveaxis(tiles, dim, 0)


def sent_and_summed(value, axis, dim):
    length = lax.axis_size(axis)
    tiles = lax.all_to_all(split_up(value, dim, length), axis, 0, 0, tiled=True)
    return jnp.sum(tiles, axis=0)


def over_axes(value, axes):
    for axis in axes:
        value = lax.psum(value, axis)
    return value


def accumulate(
    stored,
    row_list,
    col_list,
    first_slot,
    live_count,
    tile_row,
    tile_col,
    shape_info,
    row_vector,
    col_vector,
    totals,
):
    row_blocks, col_blocks, piece_blocks, grid_cols = shape_info
    vectors = row_vector.shape[0]
    block_side = stored.shape[-1]
    slot_total = stored.shape[0]
    row_pieces = row_vector.reshape(vectors, row_blocks, block_side)
    col_pieces = col_vector.reshape(vectors, col_blocks, block_side)
    offsets = jnp.arange(blocks_per_step, dtype=jnp.int32)
    row_range = jnp.arange(row_blocks, dtype=jnp.int32)
    col_range = jnp.arange(col_blocks, dtype=jnp.int32)

    def visit(group_index, running):
        row_total, col_total = running
        local_slot = group_index * blocks_per_step + offsets
        is_valid = local_slot < live_count
        slot_ids = jnp.clip(first_slot + local_slot, 0, slot_total - 1)
        tile_data = jnp.take(stored, slot_ids, axis=0)
        row_ids = jnp.take(row_list, slot_ids)
        col_ids = jnp.take(col_list, slot_ids)
        global_row = tile_row * row_blocks + row_ids
        global_col = (
            col_ids // piece_blocks * grid_cols + tile_col
        ) * piece_blocks + col_ids % piece_blocks
        mirror = is_valid & (global_row != global_col)
        col_taken = jnp.take(col_pieces, col_ids, axis=1)
        row_taken = jnp.take(row_pieces, row_ids, axis=1)
        direct = jnp.einsum(
            "gij,kgj->kgi", tile_data, col_taken, preferred_element_type=jnp.float32
        )
        turned = jnp.einsum(
            "gji,kgj->kgi", tile_data, row_taken, preferred_element_type=jnp.float32
        )
        pick_rows = ((row_ids[:, None] == row_range[None, :]) & is_valid[:, None]).astype(
            jnp.float32
        )
        pick_cols = ((col_ids[:, None] == col_range[None, :]) & mirror[:, None]).astype(jnp.float32)
        row_total = row_total + jnp.einsum(
            "gs,kgi->ksi", pick_rows, direct, precision=lax.Precision.HIGHEST
        )
        col_total = col_total + jnp.einsum(
            "gs,kgi->ksi", pick_cols, turned, precision=lax.Precision.HIGHEST
        )
        return (row_total, col_total)

    group_count = (live_count + blocks_per_step - 1) // blocks_per_step
    return lax.fori_loop(0, group_count, visit, totals)


def per_device(start_block, blocks, block_rows, block_cols, counts):
    highest = lax.Precision.HIGHEST
    vectors, piece_len = start_block.shape
    stored = blocks[0, 0]
    block_side = stored.shape[-1]
    grid_rows = lax.axis_size(ROW)
    grid_cols = lax.axis_size(COL)
    piece_blocks = piece_len // block_side
    row_blocks = grid_cols * piece_blocks
    col_blocks = grid_rows * piece_blocks
    shape_info = (row_blocks, col_blocks, piece_blocks, grid_cols)
    tile_row = lax.axis_index(ROW)
    tile_col = lax.axis_index(COL)
    row_lists = block_rows[:, 0, :]
    col_lists = block_cols[:, 0, :]
    own_count = counts[tile_row, tile_col]
    own_rows = row_lists[tile_row]
    own_cols = col_lists[tile_row]
    start_sum = over_axes(jnp.dot(start_block, start_block.T, precision=highest), ROW_COL)
    factor = jnp.linalg.cholesky(start_sum)
    current = lax.linalg.triangular_solve(factor, start_block, left_side=True, lower=True)
    previous = current
    prev_factor = factor
    diagonals = []
    couplings = []
    for step_index in range(ITERS):
        half_block = current.astype(jnp.bfloat16)
        row_vector = collect(half_block, COL, 1)
        col_vector = collect(half_block, ROW, 1)
        row_zero = jnp.zeros((vectors, row_blocks, block_side), jnp.float32)
        col_zero = jnp.zeros((vectors, col_blocks, block_side), jnp.float32)
        row_total, col_total = accumulate(
            stored,
            own_rows,
            own_cols,
            0,
            own_count,
            tile_row,
            tile_col,
            shape_info,
            row_vector,
            col_vector,
            (row_zero, col_zero),
        )
        row_part = sent_and_summed(row_total.reshape(vectors, row_blocks * block_side), COL, 1)
        col_part = sent_and_summed(col_total.reshape(vectors, col_blocks * block_side), ROW, 1)
        image = row_part + col_part
        if step_index > 0:
            image = image - jnp.dot(prev_factor.T, previous, precision=highest)
        local_proj = jnp.dot(current, image.T, precision=highest)
        local_square = jnp.dot(image, image.T, precision=highest)
        projection, squares = (over_axes(local_proj, ROW_COL), over_axes(local_square, ROW_COL))
        image = image - jnp.dot(projection.T, current, precision=highest)
        gram = squares - jnp.dot(projection.T, projection, precision=highest)
        factor = jnp.linalg.cholesky(gram)
        following = lax.linalg.triangular_solve(factor, image, left_side=True, lower=True)
        diagonals.append(projection)
        couplings.append(factor)
        previous, prev_factor, current = (current, factor, following)
    tri_size = ITERS * vectors
    tridiagonal = jnp.zeros((tri_size, tri_size), jnp.float32)
    for step_index in range(ITERS):
        low = step_index * vectors
        tridiagonal = tridiagonal.at[low : low + vectors, low : low + vectors].set(
            diagonals[step_index]
        )
        if step_index + 1 < ITERS:
            tridiagonal = tridiagonal.at[
                low : low + vectors, low + vectors : low + 2 * vectors
            ].set(couplings[step_index])
            tridiagonal = tridiagonal.at[
                low + vectors : low + 2 * vectors, low : low + vectors
            ].set(couplings[step_index].T)
    order_root = math.sqrt(piece_len * grid_rows * grid_cols)
    return (current * order_root, tridiagonal)


def solution(mesh):
    torus = Mesh(mesh.devices.reshape(4, 4, 4, 2), ("row_0", "row_1", "col_0", "col_1"))
    return jax.shard_map(
        per_device,
        mesh=torus,
        in_specs=(
            P(None, ROW_COL),
            P(ROW, COL, None, None, None),
            P(None, COL, None),
            P(None, COL, None),
            P(),
        ),
        out_specs=(P(None, ROW_COL), P()),
        check_vma=False,
    )
```

profile of v0, /device:TPU:1, one launch (start us, length us, event | category | flops | bytes accessed | tf_op | source)
XLA Modules:
  0.0 333.4 jit_solution(16994987881674295431)
XLA Ops:
  0.6 0.7 copy-done
  1.5 10.6 %psum.140 = f32[8,8]{0,1:T(8,128)S(1)} all-reduce(f32[8,8]{0,1:T(8,128)S(1)} %fusion.92), channel_id=1, replica_groups=mesh['row_0'=4,'row_1'=4,'col_0'=4,'col_1'=2] {'row_0'}, use_global_device_ids=true, to_apply=%region_0.0 | all-reduce | flops 64 | bytes 512 | tf_op jit(solution)/shard_map/psum | solution.py:47
  12.1 8.8 %psum.141 = f32[8,8]{0,1:T(8,128)S(1)} all-reduce(f32[8,8]{0,1:T(8,128)S(1)} %psum.140), channel_id=1, replica_groups=mesh['row_0'=4,'row_1'=4,'col_0'=4,'col_1'=2] {'row_1'}, use_global_device_ids=true, to_apply=%region_1.0 | all-reduce | flops 64 | bytes 512 | tf_op jit(solution)/shard_map/psum | solution.py:47
  20.9 8.7 %psum.142 = f32[8,8]{0,1:T(8,128)S(1)} all-reduce(f32[8,8]{0,1:T(8,128)S(1)} %psum.141), channel_id=1, replica_groups=mesh['row_0'=4,'row_1'=4,'col_0'=4,'col_1'=2] {'col_0'}, use_global_device_ids=true, to_apply=%region_2.0 | all-reduce | flops 64 | bytes 512 | tf_op jit(solution)/shard_map/psum | solution.py:47
  29.6 8.6 %psum.143 = f32[8,8]{0,1:T(8,128)S(1)} all-reduce(f32[8,8]{0,1:T(8,128)S(1)} %psum.142), channel_id=1, replica_groups=mesh['row_0'=4,'row_1'=4,'col_0'=4,'col_1'=2] {'col_1'}, use_global_device_ids=true, to_apply=%region_3.0 | all-reduce | flops 64 | bytes 512 | tf_op jit(solution)/shard_map/psum | solution.py:47
  38.2 0.7 cholesky.59
  41.2 8.0 %all_to_all.40 = bf16[8,8,1024]{2,1,0:T(8,128)(2,1)S(1)} all-to-all(bf16[8,8,1024]{2,1,0:T(8,128)(2,1)S(1)} %broadcast_in_dim.46), channel_id=1, replica_groups=mesh['row_0'=4,'row_1'=4,'col_0'=4,'col_1'=2] {'col_0','col_1'}, dimensions={0} | all-to-all | bytes 262144 | tf_op jit(solution)/shard_map/all_to_all | solution.py:17
  49.1 0.7 broadcast_in_dim.45
  49.9 3.5 %all-to-all-start = ((bf16[16,8,1024]{2,1,0:T(8,128)(2,1)}), bf16[16,8,1024]{2,1,0:T(8,128)(2,1)S(1)}, u32[]{:S(2)}, u32[]{:S(2)}) async-start(bf16[16,8,1024]{2,1,0:T(8,128)(2,1)} %broadcast_in_dim.45), calls=%async_computation | async-start | bytes 524288 | tf_op jit(solution)/shard_map/all_to_all | solution.py:17
  53.4 1.3 dynamic_slice.9
  55.4 0.7 dynamic-slice_bitcast_fusion
  56.1 5.2 %all-to-all-done = bf16[16,8,1024]{2,1,0:T(8,128)(2,1)S(1)} async-done(((bf16[16,8,1024]{2,1,0:T(8,128)(2,1)}), bf16[16,8,1024]{2,1,0:T(8,128)(2,1)S(1)}, u32[]{:S(2)}, u32[]{:S(2)}) %all-to-all-start) | async-done | bytes 262176 | tf_op jit(solution)/shard_map/all_to_all | solution.py:17
  61.3 8.0 %while.34 = (s32[]{:T(128)}, f32[8,64,128]{2,1,0:T(8,128)S(1)}, f32[8,128,128]{1,2,0:T(8,128)S(1)}, s32[]{:T(128)}, s32[128]{0:T(128)S(1)}, /*index=5*/bf16[8,12...) while((s32[]{:T(128)}, f32[8,64,128]{2,1,0:T(8,128)S(1)}, ...), condition=%wide.region_7.14_spmd.clone, body=%wide.region_6.13_spmd.clone.sunk | while | flops 46901184 | bytes 4142997 | solution.py:108
  64.6 2.8 gather_fusion
  68.7 0.7 fusion.142
  69.4 0.9 copy.60
  70.3 5.0 %all-to-all-start.2 = ((f32[8,8,1024]{2,1,0:T(8,128)}), f32[8,8,1024]{2,1,0:T(8,128)S(1)}, u32[]{:S(2)}, u32[]{:S(2)}) async-start(f32[8,8,1024]{2,1,0:T(8,128)} %copy.60), calls=%async_computation.2 | async-start | bytes 524288 | tf_op jit(solution)/shard_map/all_to_all | solution.py:41
  75.6 1.1 copy.62
  76.7 5.1 %all-to-all-done.2 = f32[8,8,1024]{2,1,0:T(8,128)S(1)} async-done(((f32[8,8,1024]{2,1,0:T(8,128)}), f32[8,8,1024]{2,1,0:T(8,128)S(1)}, u32[]{:S(2)}, u32[]{:S(2)}) %all-to-all-start.2) | async-done | bytes 262176 | tf_op jit(solution)/shard_map/all_to_all | solution.py:41
  81.8 58.6 %all-to-all-start.3 = ((f32[16,8,1024]{2,1,0:T(8,128)}), f32[16,8,1024]{2,1,0:T(8,128)S(1)}, u32[]{:S(2)}, u32[]{:S(2)}) async-start(f32[16,8,1024]{2,1,0:T(8,128)} %copy.62), calls=%async_computation.3 | async-start | bytes 1048576 | tf_op jit(solution)/shard_map/all_to_all | solution.py:41
  141.7 9.1 %all-to-all-done.3 = f32[16,8,1024]{2,1,0:T(8,128)S(1)} async-done(((f32[16,8,1024]{2,1,0:T(8,128)}), f32[16,8,1024]{2,1,0:T(8,128)S(1)}, u32[]{:S(2)}, u32[]{:S(2)}) %all-to-all-start.3) | async-done | bytes 524320 | tf_op jit(solution)/shard_map/all_to_all | solution.py:41
  151.1 6.7 %all-reduce.6 = (f32[8,8]{1,0:T(8,128)S(1)}, f32[8,8]{0,1:T(8,128)S(1)}) all-reduce(f32[8,8]{1,0:T(8,128)S(1)} %fusion.94, f32[8,8]{0,1:T(8,128)S(1)} %fusion.93), channel_id=1, replica_groups=mesh['row_0'=4,'row_1'=4,'col_0'=4,'col_1'=2] {'row_0'}, use_global_device_ids=true, to_apply=%region_14.21 | all-reduce | flops 128 | bytes 1024 | tf_op jit(solution)/shard_map/psum | solution.py:47
  157.9 6.7 %all-reduce.4 = (f32[8,8]{1,0:T(8,128)S(1)}, f32[8,8]{0,1:T(8,128)S(1)}) all-reduce(f32[8,8]{1,0:T(8,128)S(1)} %get-tuple-element.564, f32[8,8]{0,1:T(8,128)S(1)} %get-tuple-element.565), channel_id=1, replica_groups=mesh['row_0'=4,'row_1'=4,'col_0'=4,'col_1'=2] {'row_1'}, use_global_device_ids=true, to_apply=%region_15.22 | all-reduce | flops 128 | bytes 1024 | tf_op jit(solution)/shard_map/psum | solution.py:47
  164.5 7.0 %all-reduce.2 = (f32[8,8]{1,0:T(8,128)S(1)}, f32[8,8]{0,1:T(8,128)S(1)}) all-reduce(f32[8,8]{1,0:T(8,128)S(1)} %get-tuple-element.560, f32[8,8]{0,1:T(8,128)S(1)} %get-tuple-element.561), channel_id=1, replica_groups=mesh['row_0'=4,'row_1'=4,'col_0'=4,'col_1'=2] {'col_0'}, use_global_device_ids=true, to_apply=%region_16.23 | all-reduce | flops 128 | bytes 1024 | tf_op jit(solution)/shard_map/psum | solution.py:47
  171.5 10.3 %all-reduce.8 = (f32[8,8]{1,0:T(8,128)S(1)}, f32[8,8]{0,1:T(8,128)S(1)}) all-reduce(f32[8,8]{1,0:T(8,128)S(1)} %get-tuple-element.556, f32[8,8]{0,1:T(8,128)S(1)} %get-tuple-element.557), channel_id=1, replica_groups=mesh['row_0'=4,'row_1'=4,'col_0'=4,'col_1'=2] {'col_1'}, use_global_device_ids=true, to_apply=%region_17.24 | all-reduce | flops 128 | bytes 1024 | tf_op jit(solution)/shard_map/psum | solution.py:47
  182.4 0.7 cholesky.70
  183.1 0.7 compare_reduce_fusion.1
  183.9 2.6 fusion.83
  187.3 8.0 %all_to_all.41 = bf16[8,8,1024]{2,1,0:T(8,128)(2,1)S(1)} all-to-all(bf16[8,8,1024]{2,1,0:T(8,128)(2,1)S(1)} %broadcast_in_dim.48), channel_id=1, replica_groups=mesh['row_0'=4,'row_1'=4,'col_0'=4,'col_1'=2] {'col_0','col_1'}, dimensions={0} | all-to-all | bytes 262144 | tf_op jit(solution)/shard_map/all_to_all | solution.py:17
  195.3 0.7 broadcast_in_dim.47
  196.0 3.5 %all-to-all-start.4 = ((bf16[16,8,1024]{2,1,0:T(8,128)(2,1)}), bf16[16,8,1024]{2,1,0:T(8,128)(2,1)S(1)}, u32[]{:S(2)}, u32[]{:S(2)}) async-start(bf16[16,8,1024]{2,1,0:T(8,128)(2,1)} %broadcast_in_dim.47), calls=%async_computation.4 | async-start | bytes 524288 | tf_op jit(solution)/shard_map/all_to_all | solution.py:17
  199.6 7.9 %all-to-all-done.4 = bf16[16,8,1024]{2,1,0:T(8,128)(2,1)S(1)} async-done(((bf16[16,8,1024]{2,1,0:T(8,128)(2,1)}), bf16[16,8,1024]{2,1,0:T(8,128)(2,1)S(1)}, u32[]{:S(2)}, u32[]{:S(2)}) %all-to-all-start.4) | async-done | bytes 262176 | tf_op jit(solution)/shard_map/all_to_all | solution.py:17
  207.5 8.0 %while.35 = (s32[]{:T(128)}, f32[8,64,128]{2,1,0:T(8,128)S(1)}, f32[8,128,128]{1,2,0:T(8,128)S(1)}, s32[]{:T(128)}, s32[128]{0:T(128)S(1)}, /*index=5*/bf16[8,12...) while((s32[]{:T(128)}, f32[8,64,128]{2,1,0:T(8,128)S(1)}, ...), condition=%wide.region_19.26_spmd.clone, body=%wide.region_18.25_spmd.clone.sunk | while | flops 46901184 | bytes 4142997 | solution.py:108
  210.8 2.8 gather_fusion.5
  215.6 0.9 copy.67
  216.4 5.0 %all-to-all-start.6 = ((f32[8,8,1024]{2,1,0:T(8,128)}), f32[8,8,1024]{2,1,0:T(8,128)S(1)}, u32[]{:S(2)}, u32[]{:S(2)}) async-start(f32[8,8,1024]{2,1,0:T(8,128)} %copy.67), calls=%async_computation.6 | async-start | bytes 524288 | tf_op jit(solution)/shard_map/all_to_all | solution.py:41
  221.8 1.1 copy.69
  222.9 5.1 %all-to-all-done.6 = f32[8,8,1024]{2,1,0:T(8,128)S(1)} async-done(((f32[8,8,1024]{2,1,0:T(8,128)}), f32[8,8,1024]{2,1,0:T(8,128)S(1)}, u32[]{:S(2)}, u32[]{:S(2)}) %all-to-all-start.6) | async-done | bytes 262176 | tf_op jit(solution)/shard_map/all_to_all | solution.py:41
  228.0 58.6 %all-to-all-start.7 = ((f32[16,8,1024]{2,1,0:T(8,128)}), f32[16,8,1024]{2,1,0:T(8,128)S(1)}, u32[]{:S(2)}, u32[]{:S(2)}) async-start(f32[16,8,1024]{2,1,0:T(8,128)} %copy.69), calls=%async_computation.7 | async-start | bytes 1048576 | tf_op jit(solution)/shard_map/all_to_all | solution.py:41
  286.6 1.8 scatter.15
  288.9 8.0 %all-to-all-done.7 = f32[16,8,1024]{2,1,0:T(8,128)S(1)} async-done(((f32[16,8,1024]{2,1,0:T(8,128)}), f32[16,8,1024]{2,1,0:T(8,128)S(1)}, u32[]{:S(2)}, u32[]{:S(2)}) %all-to-all-start.7) | async-done | bytes 524320 | tf_op jit(solution)/shard_map/all_to_all | solution.py:41
  296.9 0.8 convolution_subtract_fusion.1
  298.1 6.7 %all-reduce.5 = (f32[8,8]{1,0:T(8,128)S(1)}, f32[8,8]{0,1:T(8,128)S(1)}) all-reduce(f32[8,8]{1,0:T(8,128)S(1)} %fusion.96, f32[8,8]{0,1:T(8,128)S(1)} %fusion.95), channel_id=1, replica_groups=mesh['row_0'=4,'row_1'=4,'col_0'=4,'col_1'=2] {'row_0'}, use_global_device_ids=true, to_apply=%region_26.33 | all-reduce | flops 128 | bytes 1024 | tf_op jit(solution)/shard_map/psum | solution.py:47
  304.9 6.7 %all-reduce.3 = (f32[8,8]{1,0:T(8,128)S(1)}, f32[8,8]{0,1:T(8,128)S(1)}) all-reduce(f32[8,8]{1,0:T(8,128)S(1)} %get-tuple-element.562, f32[8,8]{0,1:T(8,128)S(1)} %get-tuple-element.563), channel_id=1, replica_groups=mesh['row_0'=4,'row_1'=4,'col_0'=4,'col_1'=2] {'row_1'}, use_global_device_ids=true, to_apply=%region_27.34 | all-reduce | flops 128 | bytes 1024 | tf_op jit(solution)/shard_map/psum | solution.py:47
  311.6 7.0 %all-reduce.1 = (f32[8,8]{1,0:T(8,128)S(1)}, f32[8,8]{0,1:T(8,128)S(1)}) all-reduce(f32[8,8]{1,0:T(8,128)S(1)} %get-tuple-element.558, f32[8,8]{0,1:T(8,128)S(1)} %get-tuple-element.559), channel_id=1, replica_groups=mesh['row_0'=4,'row_1'=4,'col_0'=4,'col_1'=2] {'col_0'}, use_global_device_ids=true, to_apply=%region_28.35 | all-reduce | flops 128 | bytes 1024 | tf_op jit(solution)/shard_map/psum | solution.py:47
  318.5 10.3 %all-reduce.7 = (f32[8,8]{1,0:T(8,128)S(1)}, f32[8,8]{0,1:T(8,128)S(1)}) all-reduce(f32[8,8]{1,0:T(8,128)S(1)} %get-tuple-element.554, f32[8,8]{0,1:T(8,128)S(1)} %get-tuple-element.555), channel_id=1, replica_groups=mesh['row_0'=4,'row_1'=4,'col_0'=4,'col_1'=2] {'col_1'}, use_global_device_ids=true, to_apply=%region_29.36 | all-reduce | flops 128 | bytes 1024 | tf_op jit(solution)/shard_map/psum | solution.py:47
  329.8 0.7 cholesky.81
  332.5 0.9 convolution_multiply_fusion
  (87 shorter events, 19.5 us)
Async XLA Ops:
  0.6 0.8 copy-start
  49.9 11.4 %all-to-all-start = ((bf16[16,8,1024]{2,1,0:T(8,128)(2,1)}), bf16[16,8,1024]{2,1,0:T(8,128)(2,1)S(1)}, u32[]{:S(2)}, u32[]{:S(2)}) async-start(bf16[16,8,1024]{2,1,0:T(8,128)(2,1)} %broadcast_in_dim.45), calls=%async_computation | async-start | bytes 524288 | tf_op jit(solution)/shard_map/all_to_all | solution.py:17
  70.3 11.5 %all-to-all-start.2 = ((f32[8,8,1024]{2,1,0:T(8,128)}), f32[8,8,1024]{2,1,0:T(8,128)S(1)}, u32[]{:S(2)}, u32[]{:S(2)}) async-start(f32[8,8,1024]{2,1,0:T(8,128)} %copy.60), calls=%async_computation.2 | async-start | bytes 524288 | tf_op jit(solution)/shard_map/all_to_all | solution.py:41
  81.8 69.0 %all-to-all-start.3 = ((f32[16,8,1024]{2,1,0:T(8,128)}), f32[16,8,1024]{2,1,0:T(8,128)S(1)}, u32[]{:S(2)}, u32[]{:S(2)}) async-start(f32[16,8,1024]{2,1,0:T(8,128)} %copy.62), calls=%async_computation.3 | async-start | bytes 1048576 | tf_op jit(solution)/shard_map/all_to_all | solution.py:41
  196.0 11.4 %all-to-all-start.4 = ((bf16[16,8,1024]{2,1,0:T(8,128)(2,1)}), bf16[16,8,1024]{2,1,0:T(8,128)(2,1)S(1)}, u32[]{:S(2)}, u32[]{:S(2)}) async-start(bf16[16,8,1024]{2,1,0:T(8,128)(2,1)} %broadcast_in_dim.47), calls=%async_computation.4 | async-start | bytes 524288 | tf_op jit(solution)/shard_map/all_to_all | solution.py:17
  216.4 11.5 %all-to-all-start.6 = ((f32[8,8,1024]{2,1,0:T(8,128)}), f32[8,8,1024]{2,1,0:T(8,128)S(1)}, u32[]{:S(2)}, u32[]{:S(2)}) async-start(f32[8,8,1024]{2,1,0:T(8,128)} %copy.67), calls=%async_computation.6 | async-start | bytes 524288 | tf_op jit(solution)/shard_map/all_to_all | solution.py:41
  228.0 69.0 %all-to-all-start.7 = ((f32[16,8,1024]{2,1,0:T(8,128)}), f32[16,8,1024]{2,1,0:T(8,128)S(1)}, u32[]{:S(2)}, u32[]{:S(2)}) async-start(f32[16,8,1024]{2,1,0:T(8,128)} %copy.69), calls=%async_computation.7 | async-start | bytes 1048576 | tf_op jit(solution)/shard_map/all_to_all | solution.py:41
  329.7 3.6 %copy-start.1 = (f32[16,16]{1,0:T(8,128)}, f32[16,16]{1,0:T(8,128)S(1)}, u32[]{:S(2)}) copy-start(f32[16,16]{1,0:T(8,128)S(1)} %scatter.19) | copy-start | bytes 3076
where the time goes:
time: 335 us; the launch traced here: 333 us
  starting transfers between devices  134 us (40%)
  blocking collectives  114 us (34%)
  waiting for transfers between devices  40.4 us (12%)
  local copies, waits for them, and re-layouts  23.1 us (7%)
  other arithmetic  12.2 us (4%)
  matrix products  7.58 us (2%)
    all_to_all x4, starting transfers between devices, sent_and_summed(): tiles = lax.all_to_all(split_up(value, dim, length), axis, 0, 0, tiled=True)  127 us
    psum x12, blocking collectives, over_axes(): value = lax.psum(value, axis)  98 us
    all_to_all x4, waiting for transfers between devices, sent_and_summed(): tiles = lax.all_to_all(split_up(value, dim, length), axis, 0, 0, tiled=True)  27.3 us
    all_to_all x2, blocking collectives, sent_to_all(): lax.all_to_all(jnp.broadcast_to(value[None], (length, *value.shape)), axi...  15.9 us
    all_to_all x2, waiting for transfers between devices, sent_to_all(): lax.all_to_all(jnp.broadcast_to(value[None], (length, *value.shape)), axi...  13.1 us
    all_to_all x2, starting transfers between devices, sent_to_all(): lax.all_to_all(jnp.broadcast_to(value[None], (length, *value.shape)), axi...  7.06 us
  transfers between devices with their start and end apart: 6, of which 6 were waited for; matrix products, arithmetic and copies ran while one was open for 2% of the time, Pallas kernels for 0%

commit v1 on v0

--- a/solution.py
+++ b/solution.py
@@ -44,7 +44,7 @@
 
 def over_axes(value, axes):
     for axis in axes:
-        value = lax.psum(value, axis)
+        value = jnp.sum(lax.all_gather(value, axis), axis=0)
     return value
 
 

time: 335 us -> 438 us (1.31)
  blocking collectives: 114 us -> 213 us
    all_gather x0 -> x20, blocking collectives: none -> 196 us  [over_axes(): value = jnp.sum(lax.all_gather(value, axis), axis=0)]
    psum x12 -> x0, blocking collectives: 98 us -> none  [over_axes(): value = lax.psum(value, axis)]
where the time goes in v1:
time: 438 us; the launch traced here: 436 us
  blocking collectives  213 us (49%)
  starting transfers between devices  138 us (32%)
  waiting for transfers between devices  39.7 us (9%)
  local copies, waits for them, and re-layouts  23.2 us (5%)
  other arithmetic  12.4 us (3%)
  matrix products  7.56 us (2%)
    all_gather x20, blocking collectives, over_axes(): value = jnp.sum(lax.all_gather(value, axis), axis=0)  196 us
    all_to_all x4, starting transfers between devices, sent_and_summed(): tiles = lax.all_to_all(split_up(value, dim, length), axis, 0, 0, tiled=True)  128 us
    all_to_all x4, waiting for transfers between devices, sent_and_summed(): tiles = lax.all_to_all(split_up(value, dim, length), axis, 0, 0, tiled=True)  27.3 us
    all_to_all x2, blocking collectives, sent_to_all(): lax.all_to_all(jnp.broadcast_to(value[None], (length, *value.shape)), axi...  17.3 us
    all_to_all x2, waiting for transfers between devices, sent_to_all(): lax.all_to_all(jnp.broadcast_to(value[None], (length, *value.shape)), axi...  12.4 us
    all_to_all x2, starting transfers between devices, sent_to_all(): lax.all_to_all(jnp.broadcast_to(value[None], (length, *value.shape)), axi...  9.31 us
  transfers between devices with their start and end apart: 6, of which 6 were waited for; matrix products, arithmetic and copies ran while one was open for 2% of the time, Pallas kernels for 0%

profile of v1, /device:TPU:1, one launch (start us, length us, event | category | flops | bytes accessed | tf_op | source)
XLA Modules:
  0.0 435.6 jit_solution(1910977513170912685)
XLA Ops:
  0.6 0.7 copy-done
  1.5 11.2 %all-gather = f32[32,8]{1,0:T(8,128)S(1)} all-gather(f32[8,8]{1,0:T(8,128)S(1)} %fusion.92), channel_id=2, replica_groups=mesh['row_0'=4,'row_1'=4,'col_0'=4,'col_1'=2] {'row_0'}, dimensions={0}, use_global_device_ids=true | all-gather | bytes 1280 | tf_op jit(solution)/shard_map/all_gather | solution.py:47
  12.7 9.5 %all-gather.1 = f32[32,8]{1,0:T(8,128)S(1)} all-gather(f32[8,8]{1,0:T(8,128)S(1)} %bitcast_reduce_fusion.14), channel_id=3, replica_groups=mesh['row_0'=4,'row_1'=4,'col_0'=4,'col_1'=2] {'row_1'}, dimensions={0}, use_global_device_ids=true | all-gather | bytes 1280 | tf_op jit(solution)/shard_map/all_gather | solution.py:47
  22.2 9.6 %all-gather.2 = f32[32,8]{1,0:T(8,128)S(1)} all-gather(f32[8,8]{1,0:T(8,128)S(1)} %bitcast_reduce_fusion.13), channel_id=4, replica_groups=mesh['row_0'=4,'row_1'=4,'col_0'=4,'col_1'=2] {'col_0'}, dimensions={0}, use_global_device_ids=true | all-gather | bytes 1280 | tf_op jit(solution)/shard_map/all_gather | solution.py:47
  31.8 10.8 %all-gather.3 = f32[16,8]{1,0:T(8,128)S(1)} all-gather(f32[8,8]{1,0:T(8,128)S(1)} %bitcast_reduce_fusion.12), channel_id=5, replica_groups=mesh['row_0'=4,'row_1'=4,'col_0'=4,'col_1'=2] {'col_1'}, dimensions={0}, use_global_device_ids=true | all-gather | bytes 768 | tf_op jit(solution)/shard_map/all_gather | solution.py:47
  45.6 9.2 %all_to_all.40 = bf16[8,8,1024]{2,1,0:T(8,128)(2,1)S(1)} all-to-all(bf16[8,8,1024]{2,1,0:T(8,128)(2,1)S(1)} %broadcast_in_dim.46), channel_id=1, replica_groups=mesh['row_0'=4,'row_1'=4,'col_0'=4,'col_1'=2] {'col_0','col_1'}, dimensions={0} | all-to-all | bytes 262144 | tf_op jit(solution)/shard_map/all_to_all | solution.py:17
  55.5 5.8 %all-to-all-start = ((bf16[16,8,1024]{2,1,0:T(8,128)(2,1)}), bf16[16,8,1024]{2,1,0:T(8,128)(2,1)S(1)}, u32[]{:S(2)}, u32[]{:S(2)}) async-start(bf16[16,8,1024]{2,1,0:T(8,128)(2,1)} %broadcast_in_dim.45), calls=%async_computation | async-start | bytes 524288 | tf_op jit(solution)/shard_map/all_to_all | solution.py:17
  61.3 1.3 dynamic_slice.9
  64.0 4.9 %all-to-all-done = bf16[16,8,1024]{2,1,0:T(8,128)(2,1)S(1)} async-done(((bf16[16,8,1024]{2,1,0:T(8,128)(2,1)}), bf16[16,8,1024]{2,1,0:T(8,128)(2,1)S(1)}, u32[]{:S(2)}, u32[]{:S(2)}) %all-to-all-start) | async-done | bytes 262176 | tf_op jit(solution)/shard_map/all_to_all | solution.py:17
  69.0 8.0 %while.34 = (s32[]{:T(128)}, f32[8,64,128]{2,1,0:T(8,128)S(1)}, f32[8,128,128]{1,2,0:T(8,128)S(1)}, s32[]{:T(128)}, s32[128]{0:T(128)S(1)}, /*index=5*/bf16[8,12...) while((s32[]{:T(128)}, f32[8,64,128]{2,1,0:T(8,128)S(1)}, ...), condition=%wide.region_7.14_spmd.clone, body=%wide.region_6.13_spmd.clone.sunk | while | flops 46901184 | bytes 4142997 | solution.py:108
  72.2 2.8 gather_fusion
  77.0 0.9 copy.84
  77.9 5.6 %all-to-all-start.2 = ((f32[8,8,1024]{2,1,0:T(8,128)}), f32[8,8,1024]{2,1,0:T(8,128)S(1)}, u32[]{:S(2)}, u32[]{:S(2)}) async-start(f32[8,8,1024]{2,1,0:T(8,128)} %copy.84), calls=%async_computation.2 | async-start | bytes 524288 | tf_op jit(solution)/shard_map/all_to_all | solution.py:41
  83.7 1.1 copy.86
  84.8 5.1 %all-to-all-done.2 = f32[8,8,1024]{2,1,0:T(8,128)S(1)} async-done(((f32[8,8,1024]{2,1,0:T(8,128)}), f32[8,8,1024]{2,1,0:T(8,128)S(1)}, u32[]{:S(2)}, u32[]{:S(2)}) %all-to-all-start.2) | async-done | bytes 262176 | tf_op jit(solution)/shard_map/all_to_all | solution.py:41
  89.9 58.6 %all-to-all-start.3 = ((f32[16,8,1024]{2,1,0:T(8,128)}), f32[16,8,1024]{2,1,0:T(8,128)S(1)}, u32[]{:S(2)}, u32[]{:S(2)}) async-start(f32[16,8,1024]{2,1,0:T(8,128)} %copy.86), calls=%async_computation.3 | async-start | bytes 1048576 | tf_op jit(solution)/shard_map/all_to_all | solution.py:41
  149.9 9.1 %all-to-all-done.3 = f32[16,8,1024]{2,1,0:T(8,128)S(1)} async-done(((f32[16,8,1024]{2,1,0:T(8,128)}), f32[16,8,1024]{2,1,0:T(8,128)S(1)}, u32[]{:S(2)}, u32[]{:S(2)}) %all-to-all-start.3) | async-done | bytes 524320 | tf_op jit(solution)/shard_map/all_to_all | solution.py:41
  159.3 9.2 %all-gather.4 = f32[32,8]{1,0:T(8,128)S(1)} all-gather(f32[8,8]{1,0:T(8,128)S(1)} %fusion.93), channel_id=6, replica_groups=mesh['row_0'=4,'row_1'=4,'col_0'=4,'col_1'=2] {'row_0'}, dimensions={0}, use_global_device_ids=true | all-gather | bytes 1280 | tf_op jit(solution)/shard_map/all_gather | solution.py:47
  168.5 9.1 %all-gather.5 = f32[32,8]{1,0:T(8,128)S(1)} all-gather(f32[8,8]{1,0:T(8,128)S(1)} %bitcast_reduce_fusion.11), channel_id=7, replica_groups=mesh['row_0'=4,'row_1'=4,'col_0'=4,'col_1'=2] {'row_1'}, dimensions={0}, use_global_device_ids=true | all-gather | bytes 1280 | tf_op jit(solution)/shard_map/all_gather | solution.py:47
  177.6 9.1 %all-gather.6 = f32[32,8]{1,0:T(8,128)S(1)} all-gather(f32[8,8]{1,0:T(8,128)S(1)} %bitcast_reduce_fusion.10), channel_id=8, replica_groups=mesh['row_0'=4,'row_1'=4,'col_0'=4,'col_1'=2] {'col_0'}, dimensions={0}, use_global_device_ids=true | all-gather | bytes 1280 | tf_op jit(solution)/shard_map/all_gather | solution.py:47
  186.7 12.3 %all-gather.7 = f32[16,8]{1,0:T(8,128)S(1)} all-gather(f32[8,8]{1,0:T(8,128)S(1)} %bitcast_reduce_fusion.9), channel_id=9, replica_groups=mesh['row_0'=4,'row_1'=4,'col_0'=4,'col_1'=2] {'col_1'}, dimensions={0}, use_global_device_ids=true | all-gather | bytes 768 | tf_op jit(solution)/shard_map/all_gather | solution.py:47
  199.1 9.1 %all-gather.8 = f32[32,8]{1,0:T(8,128)S(1)} all-gather(f32[8,8]{1,0:T(8,128)S(1)} %fusion.94), channel_id=10, replica_groups=mesh['row_0'=4,'row_1'=4,'col_0'=4,'col_1'=2] {'row_0'}, dimensions={0}, use_global_device_ids=true | all-gather | bytes 1280 | tf_op jit(solution)/shard_map/all_gather | solution.py:47
  208.2 9.1 %all-gather.9 = f32[32,8]{1,0:T(8,128)S(1)} all-gather(f32[8,8]{1,0:T(8,128)S(1)} %bitcast_reduce_fusion.8), channel_id=11, replica_groups=mesh['row_0'=4,'row_1'=4,'col_0'=4,'col_1'=2] {'row_1'}, dimensions={0}, use_global_device_ids=true | all-gather | bytes 1280 | tf_op jit(solution)/shard_map/all_gather | solution.py:47
  217.3 9.1 %all-gather.10 = f32[32,8]{1,0:T(8,128)S(1)} all-gather(f32[8,8]{1,0:T(8,128)S(1)} %bitcast_reduce_fusion.7), channel_id=12, replica_groups=mesh['row_0'=4,'row_1'=4,'col_0'=4,'col_1'=2] {'col_0'}, dimensions={0}, use_global_device_ids=true | all-gather | bytes 1280 | tf_op jit(solution)/shard_map/all_gather | solution.py:47
  226.5 10.5 %all-gather.11 = f32[16,8]{1,0:T(8,128)S(1)} all-gather(f32[8,8]{1,0:T(8,128)S(1)} %bitcast_reduce_fusion.6), channel_id=13, replica_groups=mesh['row_0'=4,'row_1'=4,'col_0'=4,'col_1'=2] {'col_1'}, dimensions={0}, use_global_device_ids=true | all-gather | bytes 768 | tf_op jit(solution)/shard_map/all_gather | solution.py:47
  238.9 2.6 fusion.83
  242.4 8.1 %all_to_all.41 = bf16[8,8,1024]{2,1,0:T(8,128)(2,1)S(1)} all-to-all(bf16[8,8,1024]{2,1,0:T(8,128)(2,1)S(1)} %broadcast_in_dim.48), channel_id=1, replica_groups=mesh['row_0'=4,'row_1'=4,'col_0'=4,'col_1'=2] {'col_0','col_1'}, dimensions={0} | all-to-all | bytes 262144 | tf_op jit(solution)/shard_map/all_to_all | solution.py:17
  251.2 3.5 all-to-all-start.4
  254.8 7.5 %all-to-all-done.4 = bf16[16,8,1024]{2,1,0:T(8,128)(2,1)S(1)} async-done(((bf16[16,8,1024]{2,1,0:T(8,128)(2,1)}), bf16[16,8,1024]{2,1,0:T(8,128)(2,1)S(1)}, u32[]{:S(2)}, u32[]{:S(2)}) %all-to-all-start.4) | async-done | bytes 262176 | tf_op jit(solution)/shard_map/all_to_all | solution.py:17
  262.3 8.0 %while.35 = (s32[]{:T(128)}, f32[8,64,128]{2,1,0:T(8,128)S(1)}, f32[8,128,128]{1,2,0:T(8,128)S(1)}, s32[]{:T(128)}, s32[128]{0:T(128)S(1)}, /*index=5*/bf16[8,12...) while((s32[]{:T(128)}, f32[8,64,128]{2,1,0:T(8,128)S(1)}, ...), condition=%wide.region_19.26_spmd.clone, body=%wide.region_18.25_spmd.clone.sunk | while | flops 46901184 | bytes 4142997 | solution.py:108
  265.6 2.8 gather_fusion.5
  270.4 0.9 copy.92
  271.3 5.6 %all-to-all-start.6 = ((f32[8,8,1024]{2,1,0:T(8,128)}), f32[8,8,1024]{2,1,0:T(8,128)S(1)}, u32[]{:S(2)}, u32[]{:S(2)}) async-start(f32[8,8,1024]{2,1,0:T(8,128)} %copy.92), calls=%async_computation.6 | async-start | bytes 524288 | tf_op jit(solution)/shard_map/all_to_all | solution.py:41
  277.1 1.1 copy.94
  278.2 5.1 %all-to-all-done.6 = f32[8,8,1024]{2,1,0:T(8,128)S(1)} async-done(((f32[8,8,1024]{2,1,0:T(8,128)}), f32[8,8,1024]{2,1,0:T(8,128)S(1)}, u32[]{:S(2)}, u32[]{:S(2)}) %all-to-all-start.6) | async-done | bytes 262176 | tf_op jit(solution)/shard_map/all_to_all | solution.py:41
  283.3 58.6 %all-to-all-start.7 = ((f32[16,8,1024]{2,1,0:T(8,128)}), f32[16,8,1024]{2,1,0:T(8,128)S(1)}, u32[]{:S(2)}, u32[]{:S(2)}) async-start(f32[16,8,1024]{2,1,0:T(8,128)} %copy.94), calls=%async_computation.7 | async-start | bytes 1048576 | tf_op jit(solution)/shard_map/all_to_all | solution.py:41
  342.1 1.8 scatter.15
  344.3 8.0 %all-to-all-done.7 = f32[16,8,1024]{2,1,0:T(8,128)S(1)} async-done(((f32[16,8,1024]{2,1,0:T(8,128)}), f32[16,8,1024]{2,1,0:T(8,128)S(1)}, u32[]{:S(2)}, u32[]{:S(2)}) %all-to-all-start.7) | async-done | bytes 524320 | tf_op jit(solution)/shard_map/all_to_all | solution.py:41
  352.4 0.8 convolution_subtract_fusion.1
  353.6 9.2 %all-gather.12 = f32[32,8]{1,0:T(8,128)S(1)} all-gather(f32[8,8]{1,0:T(8,128)S(1)} %fusion.95), channel_id=14, replica_groups=mesh['row_0'=4,'row_1'=4,'col_0'=4,'col_1'=2] {'row_0'}, dimensions={0}, use_global_device_ids=true | all-gather | bytes 1280 | tf_op jit(solution)/shard_map/all_gather | solution.py:47
  362.7 9.1 %all-gather.13 = f32[32,8]{1,0:T(8,128)S(1)} all-gather(f32[8,8]{1,0:T(8,128)S(1)} %bitcast_reduce_fusion.5), channel_id=15, replica_groups=mesh['row_0'=4,'row_1'=4,'col_0'=4,'col_1'=2] {'row_1'}, dimensions={0}, use_global_device_ids=true | all-gather | bytes 1280 | tf_op jit(solution)/shard_map/all_gather | solution.py:47
  371.8 9.1 %all-gather.14 = f32[32,8]{1,0:T(8,128)S(1)} all-gather(f32[8,8]{1,0:T(8,128)S(1)} %bitcast_reduce_fusion.4), channel_id=16, replica_groups=mesh['row_0'=4,'row_1'=4,'col_0'=4,'col_1'=2] {'col_0'}, dimensions={0}, use_global_device_ids=true | all-gather | bytes 1280 | tf_op jit(solution)/shard_map/all_gather | solution.py:47
  381.0 12.3 %all-gather.15 = f32[16,8]{1,0:T(8,128)S(1)} all-gather(f32[8,8]{1,0:T(8,128)S(1)} %bitcast_reduce_fusion.3), channel_id=17, replica_groups=mesh['row_0'=4,'row_1'=4,'col_0'=4,'col_1'=2] {'col_1'}, dimensions={0}, use_global_device_ids=true | all-gather | bytes 768 | tf_op jit(solution)/shard_map/all_gather | solution.py:47
  393.3 9.1 %all-gather.16 = f32[32,8]{1,0:T(8,128)S(1)} all-gather(f32[8,8]{1,0:T(8,128)S(1)} %fusion.96), channel_id=18, replica_groups=mesh['row_0'=4,'row_1'=4,'col_0'=4,'col_1'=2] {'row_0'}, dimensions={0}, use_global_device_ids=true | all-gather | bytes 1280 | tf_op jit(solution)/shard_map/all_gather | solution.py:47
  402.4 9.1 %all-gather.17 = f32[32,8]{1,0:T(8,128)S(1)} all-gather(f32[8,8]{1,0:T(8,128)S(1)} %bitcast_reduce_fusion.2), channel_id=19, replica_groups=mesh['row_0'=4,'row_1'=4,'col_0'=4,'col_1'=2] {'row_1'}, dimensions={0}, use_global_device_ids=true | all-gather | bytes 1280 | tf_op jit(solution)/shard_map/all_gather | solution.py:47
  411.6 9.1 %all-gather.18 = f32[32,8]{1,0:T(8,128)S(1)} all-gather(f32[8,8]{1,0:T(8,128)S(1)} %bitcast_reduce_fusion.1), channel_id=20, replica_groups=mesh['row_0'=4,'row_1'=4,'col_0'=4,'col_1'=2] {'col_0'}, dimensions={0}, use_global_device_ids=true | all-gather | bytes 1280 | tf_op jit(solution)/shard_map/all_gather | solution.py:47
  420.7 10.5 %all-gather.19 = f32[16,8]{1,0:T(8,128)S(1)} all-gather(f32[8,8]{1,0:T(8,128)S(1)} %bitcast_reduce_fusion), channel_id=21, replica_groups=mesh['row_0'=4,'row_1'=4,'col_0'=4,'col_1'=2] {'col_1'}, dimensions={0}, use_global_device_ids=true | all-gather | bytes 768 | tf_op jit(solution)/shard_map/all_gather | solution.py:47
  434.8 0.9 convolution_multiply_fusion
  (117 shorter events, 25.3 us)
Async XLA Ops:
  0.6 0.8 copy-start
  55.5 13.4 %all-to-all-start = ((bf16[16,8,1024]{2,1,0:T(8,128)(2,1)}), bf16[16,8,1024]{2,1,0:T(8,128)(2,1)S(1)}, u32[]{:S(2)}, u32[]{:S(2)}) async-start(bf16[16,8,1024]{2,1,0:T(8,128)(2,1)} %broadcast_in_dim.45), calls=%async_computation | async-start | bytes 524288 | tf_op jit(solution)/shard_map/all_to_all | solution.py:17
  77.9 12.1 %all-to-all-start.2 = ((f32[8,8,1024]{2,1,0:T(8,128)}), f32[8,8,1024]{2,1,0:T(8,128)S(1)}, u32[]{:S(2)}, u32[]{:S(2)}) async-start(f32[8,8,1024]{2,1,0:T(8,128)} %copy.84), calls=%async_computation.2 | async-start | bytes 524288 | tf_op jit(solution)/shard_map/all_to_all | solution.py:41
  89.9 69.0 %all-to-all-start.3 = ((f32[16,8,1024]{2,1,0:T(8,128)}), f32[16,8,1024]{2,1,0:T(8,128)S(1)}, u32[]{:S(2)}, u32[]{:S(2)}) async-start(f32[16,8,1024]{2,1,0:T(8,128)} %copy.86), calls=%async_computation.3 | async-start | bytes 1048576 | tf_op jit(solution)/shard_map/all_to_all | solution.py:41
  251.2 11.1 %all-to-all-start.4 = ((bf16[16,8,1024]{2,1,0:T(8,128)(2,1)}), bf16[16,8,1024]{2,1,0:T(8,128)(2,1)S(1)}, u32[]{:S(2)}, u32[]{:S(2)}) async-start(bf16[16,8,1024]{2,1,0:T(8,128)(2,1)} %broadcast_in_dim.47), calls=%async_computation.4 | async-start | bytes 524288 | tf_op jit(solution)/shard_map/all_to_all | solution.py:17
  271.3 12.1 %all-to-all-start.6 = ((f32[8,8,1024]{2,1,0:T(8,128)}), f32[8,8,1024]{2,1,0:T(8,128)S(1)}, u32[]{:S(2)}, u32[]{:S(2)}) async-start(f32[8,8,1024]{2,1,0:T(8,128)} %copy.92), calls=%async_computation.6 | async-start | bytes 524288 | tf_op jit(solution)/shard_map/all_to_all | solution.py:41
  283.3 69.0 %all-to-all-start.7 = ((f32[16,8,1024]{2,1,0:T(8,128)}), f32[16,8,1024]{2,1,0:T(8,128)S(1)}, u32[]{:S(2)}, u32[]{:S(2)}) async-start(f32[16,8,1024]{2,1,0:T(8,128)} %copy.94), calls=%async_computation.7 | async-start | bytes 1048576 | tf_op jit(solution)/shard_map/all_to_all | solution.py:41
  432.0 3.6 copy-start.1
